TPU v7x, 256 devices: a whole 4x4x8 slice. The times are simulated.
256 devices in a mesh: row: 16 (over z, core), col: 16 (over x, y).
Axes of the slice: x: 4, y: 4, z: 8, core: 2. Of those that a mesh axis runs over, the one named last changes fastest.
Arguments:
- genotypes: int32 [4096, 16384], P(('row', 'col')), may hold values from 0 to 2, as said below
- snp_index: int32 [4096], P(('row', 'col')), may hold values from 0 to 16383, as said below
- freq_table: float32 [16384], replicated, as said below
- prior: float32 [16384, 16384], P('row', 'col'), as said below
- start_vectors: float32 [16384, 20], P('row'), may hold values from -6 to 6
Outputs:
- grm: float32 [16384, 16384], P('row', 'col')
- pcs: float32 [16384, 20], P('col')
- spectrum: float32 [3, 20], replicated
Inputs may be any that keep to these rules, and one draw needn't show every extreme that they name: `genotypes`: genotype dosages 0, 1 or 2. `snp_index`: strictly increasing; entry j lies in 4 * j to 4 * j + 3. `freq_table`: frequencies are multiples of 1/1024 between 52/1024 and 512/1024. `prior`: exactly symmetric; diagonal between 1 and 2, off-diagonal entries small.
All inputs are finite; a program needn't handle non-finite values.
Results may differ from a plain program's by a relative error of at most 0.0075.
Values may be sent and summed in bfloat16 or wider, within the bound.
No kernel may reach another device: no remote copies, remote signals or barrier semaphores. Data moves between devices by JAX's collectives and lax.ppermute only.
A program may use at most 128 MiB of HBM per device.

v0:
```python
import jax
import jax.numpy as jnp
from jax import lax
from jax.sharding import Mesh
from jax.sharding import PartitionSpec as P

S = 16384
ITERS = 3
COL = ("col_0", "col_1")
ROW_COL = ("row", "col_0", "col_1")


def total_of_pieces(array, axis):
    return lax.all_gather(array, axis).sum(0)


def copy_for_each(array, axis):
    length = lax.axis_size(axis)
    return lax.all_to_all(
        jnp.broadcast_to(array[None], (length, *array.shape)), axis, 0, 0, tiled=True
    )


def taken_together(array, axis):
    return copy_for_each(array, axis).sum(axis=0)


def in_one(arrays, axis):
    ravelled, at, outs = (jnp.concatenate([a.reshape(-1) for a in arrays]), 0, [])
    so_far = taken_together(ravelled, axis)
    for a in arrays:
        outs.append(so_far[at : at + a.size].reshape(a.shape))
        at += a.size
    return tuple(outs)


def one_axis_at_a_time(array, axes):
    for axis in axes:
        array = lax.psum(array, axis)
    return array


def standardize(genotypes, allele_freq):
    doubled = 2.0 * allele_freq
    spread = jnp.sqrt(doubled * (1.0 - allele_freq))
    return (genotypes.astype(jnp.float32) - doubled[:, None]) / spread[:, None]


def orthonormal(factor, image):
    return lax.linalg.triangular_solve(factor, image, left_side=False, lower=True, transpose_a=True)


def apply_tile(tile, vectors, transposed):
    if transposed:
        return lax.dot_general(tile, vectors, (((0,), (0,)), ((), ())))
    return jnp.dot(tile, vectors)


def local_gram(image):
    return jnp.dot(image.T, image)


def body(genotypes, snp_index, freq_table, prior, start_vectors):
    allele_freq = jnp.take(freq_table, snp_index)
    standard = standardize(genotypes, allele_freq).astype(jnp.bfloat16)
    row_count = lax.axis_size("row")
    col_count = lax.axis_size(COL)
    own_snps = genotypes.shape[0]
    total_snps = own_snps * row_count * col_count
    row_piece = lax.all_to_all(standard, "row", split_axis=1, concat_axis=0, tiled=True)
    col_piece = lax.all_to_all(standard, COL, split_axis=1, concat_axis=0, tiled=True)
    col_piece = col_piece.reshape(col_count, 1, own_snps, col_piece.shape[1])
    col_panel = lax.all_gather(col_piece, "row", axis=1, tiled=True)
    col_panel = col_panel.reshape(total_snps, col_panel.shape[3])
    window = lax.dot_general(
        lax.all_gather(row_piece, COL, axis=0, tiled=True),
        col_panel,
        (((0,), (0,)), ((), ())),
        preferred_element_type=jnp.float32,
    )
    grm = prior + window / total_snps
    scaled_start = start_vectors / jnp.sqrt(jnp.float32(S))
    diagonals = []
    image = total_of_pieces(apply_tile(grm, scaled_start, True), "row")
    for step in range(1, ITERS):
        if step % 2 == 1:
            product, gram = in_one((apply_tile(grm, image, False), local_gram(image)), COL)
        else:
            product, gram = (
                total_of_pieces(apply_tile(grm, image, True), "row"),
                total_of_pieces(local_gram(image), "row"),
            )
        factor = jnp.linalg.cholesky(gram)
        diagonals.append(jnp.diagonal(factor))
        image = orthonormal(factor, product)
    gram = one_axis_at_a_time(local_gram(image), COL)
    factor = jnp.linalg.cholesky(gram)
    diagonals.append(jnp.diagonal(factor))
    vectors = orthonormal(factor, image)
    pcs = vectors * jnp.sqrt(jnp.float32(S))
    spectrum = jnp.stack(diagonals, axis=0)
    return (grm, pcs, spectrum)


def solution(mesh):
    finer = Mesh(mesh.devices.reshape(mesh.shape["row"], 4, 4), ("row", "col_0", "col_1"))
    in_specs = (P(ROW_COL, None), P(ROW_COL), P(), P("row", COL), P("row", None))
    out_specs = (P("row", COL), P(COL, None), P())
    return jax.shard_map(body, mesh=finer, in_specs=in_specs, out_specs=out_specs, check_vma=False)
```

profile of v0, /device:TPU:32, one launch (start us, length us, event | category | flops | bytes accessed | tf_op | source)
XLA Modules:
  0.0 351.4 jit_solution(14662210511644327606)
XLA Ops:
  9.3 1.4 divide_convert_fusion
  10.8 18.3 %all_to_all.38 = bf16[16,16,1024]{2,0,1:T(8,128)(2,1)S(1)} all-to-all(bf16[16,16,1024]{2,0,1:T(8,128)(2,1)S(1)} %bitcast.82), channel_id=1, replica_groups=mesh['row'=16,'col_0'=4,'col_1'=4] {'col_0','col_1'}, dimensions={1} | all-to-all | bytes 1048576 | tf_op jit(solution)/shard_map/all_to_all | solution.py:71
  29.1 1.1 copy.44
  30.3 25.6 %all_to_all.39 = bf16[16,16,1024]{2,0,1:T(8,128)(2,1)} all-to-all(bf16[16,16,1024]{2,0,1:T(8,128)(2,1)S(1)} %bitcast.83), channel_id=1, replica_groups=mesh['row'=16,'col_0'=4,'col_1'=4] {'row'}, dimensions={1} | all-to-all | bytes 1048576 | tf_op jit(solution)/shard_map/all_to_all | solution.py:70
  55.9 37.5 %all-gather.12.cloned.1.call-done = bf16[16,256,1024]{2,0,1:T(8,128)(2,1)} async-done(((bf16[16,16,1024]{2,0,1:T(8,128)(2,1)}), bf16[16,256,1024]{2,0,1:T(8,128)(2,1)}) %all-gather.12.cloned.1.call-update) | async-done | bytes 8388624 | tf_op jit(solution)/shard_map/all_gather | solution.py:73
  93.5 11.3 %copy.45 = bf16[16,256,1024]{2,1,0:T(8,128)(2,1)} copy(bf16[16,256,1024]{2,0,1:T(8,128)(2,1)} %all-gather.12.cloned.1.call-done) | data formatting | bytes 16777216 | tf_op jit(solution)/shard_map/all_gather | solution.py:73
  104.8 63.9 %all-gather.10.cloned.1.call-done = bf16[4096,1024]{1,0:T(8,128)(2,1)} async-done(((bf16[256,1024]{1,0:T(8,128)(2,1)}), bf16[4096,1024]{1,0:T(8,128)(2,1)}) %all-gather.10.cloned.1.call-update) | async-done | bytes 8388624 | tf_op jit(solution)/shard_map/all_gather | solution.py:76
  168.6 14.4 %multiply_add_fusion = f32[1024,1024]{1,0:T(8,128)S(1)} fusion(f32[1024,1024]{1,0:T(8,128)} %param.11, bf16[4096,1024]{1,0:T(8,128)(2,1)} %all-gather.10.cloned.1.call-done, bf16[4096,1024]{1,0:T(8,128)(2,1)} %bitcast.79), kind=kOutput, calls=%fused_computation.4 | convolution fusion | flops 8592031744 | bytes 25165824 | tf_op jit(solution)/shard_map/dot_general | solution.py:75
  183.0 2.0 copy-done.1
  186.3 38.1 %all-gather.14.cloned.1.call-done = f32[16384,20]{0,1:T(8,128)} async-done(((f32[1024,20]{0,1:T(8,128)}), f32[16384,20]{0,1:T(8,128)}) %all-gather.14.cloned.1.call-update) | async-done | bytes 1310736 | tf_op jit(solution)/shard_map/all_gather | solution.py:14
  224.4 2.5 copy.58
  229.2 27.1 %all_to_all.40 = f32[16,1,20880]{2,1,0:T(1,128)S(1)} all-to-all(f32[16,1,20880]{2,1,0:T(1,128)S(1)} %broadcast_in_dim.22), channel_id=1, replica_groups=mesh['row'=16,'col_0'=4,'col_1'=4] {'col_0','col_1'}, dimensions={0} | all-to-all | bytes 2672640 | tf_op jit(solution)/shard_map/all_to_all | solution.py:19
  257.3 1.8 cholesky.59
  260.5 1.5 custom-call.13
  263.2 3.2 fusion.27
  266.6 15.7 %all-gather.4 = f32[16,20,20]{2,1,0:T(8,128)S(1)} all-gather(f32[1,20,20]{2,1,0:T(8,128)S(1)} %convolution_bitcast_fusion.3), channel_id=4, replica_groups=mesh['row'=16,'col_0'=4,'col_1'=4] {'row'}, dimensions={0}, use_global_device_ids=true | all-gather | bytes 27200 | tf_op jit(solution)/shard_map/all_gather | solution.py:14
  282.4 1.8 cholesky.70
  285.6 1.5 custom-call.14
  288.7 12.4 %all-gather.16.cloned.1.call-done = f32[16384,20]{0,1:T(8,128)} async-done(((f32[1024,20]{0,1:T(8,128)}), f32[16384,20]{0,1:T(8,128)}) %all-gather.16.cloned.1.call-update) | async-done | bytes 1310736 | tf_op jit(solution)/shard_map/all_gather | solution.py:14
  301.1 2.3 copy.59
  304.1 16.8 %psum.14 = f32[20,20]{0,1:T(8,128)S(1)} all-reduce(f32[20,20]{0,1:T(8,128)S(1)} %fusion.28), channel_id=1, replica_groups=mesh['row'=16,'col_0'=4,'col_1'=4] {'col_0'}, use_global_device_ids=true, to_apply=%region_6.9 | all-reduce | flops 400 | bytes 3200 | tf_op jit(solution)/shard_map/psum | solution.py:39
  320.9 16.8 %psum.15 = f32[20,20]{0,1:T(8,128)S(1)} all-reduce(f32[20,20]{0,1:T(8,128)S(1)} %psum.14), channel_id=1, replica_groups=mesh['row'=16,'col_0'=4,'col_1'=4] {'col_1'}, use_global_device_ids=true, to_apply=%region_7.10 | all-reduce | flops 400 | bytes 3200 | tf_op jit(solution)/shard_map/psum | solution.py:39
  337.8 1.8 cholesky.81
  341.8 1.5 custom-call.15
  (61 shorter events, 17.0 us)
Async XLA Ops:
  7.2 0.8 copy-start
  7.2 86.3 %all-gather.12.cloned.1.call-start = ((), (), s32[]{:S(2)}) async-start(), calls=%async_computation.4 | async-start | bytes 8912896 | tf_op jit(solution)/shard_map/all_gather | solution.py:73
  30.2 138.4 %all-gather.10.cloned.1.call-start = ((), (), s32[]{:S(2)}) async-start(), calls=%async_computation.3 | async-start | bytes 8912896 | tf_op jit(solution)/shard_map/all_gather | solution.py:76
  55.9 168.6 %all-gather.14.cloned.1.call-start = ((), (), s32[]{:S(2)}) async-start(), calls=%async_computation.5 | async-start | bytes 1671168 | tf_op jit(solution)/shard_map/all_gather | solution.py:14
  168.6 16.4 %copy-start.3 = (f32[1024,20]{0,1:T(8,128)S(1)}, f32[1024,20]{0,1:T(8,128)}, u32[]{:S(2)}) copy-start(f32[1024,20]{0,1:T(8,128)} %param.12) | copy-start | bytes 245764
  183.0 2.0 copy-start.1
  186.1 115.0 %all-gather.16.cloned.1.call-start = ((), (), s32[]{:S(2)}) async-start(), calls=%async_computation.6 | async-start | bytes 1671168 | tf_op jit(solution)/shard_map/all_gather | solution.py:14
  224.4 2.7 copy-start.2
Sparse Core Ops, SparseCore 0:
  30.4 63.0 all-gather.11
  95.9 72.6 all-gather.9
  186.2 38.1 all-gather.13
  266.6 34.5 all-gather.15
where the time goes:
time: 352 us; the launch traced here: 351 us
  waiting for transfers between devices  152 us (43%)
  blocking collectives  120 us (34%)
  local copies, waits for them, and re-layouts  24.6 us (7%)
  matrix products  21.5 us (6%)
  other arithmetic  18.7 us (5%)
  between operations  13.9 us (4%)
    all_gather x1, waiting for transfers between devices, body(): lax.all_gather(row_piece, COL, axis=0, tiled=True)  63.9 us
    all_gather x2, waiting for transfers between devices, total_of_pieces(): return lax.all_gather(array, axis).sum(0)  50.5 us
    all_gather x1, waiting for transfers between devices, body(): col_panel = lax.all_gather(col_piece, 'row', axis=1, tiled=True)  37.5 us
    psum x2, blocking collectives, one_axis_at_a_time(): array = lax.psum(array, axis)  33.6 us
    all_to_all x1, blocking collectives, copy_for_each(): lax.all_to_all(jnp.broadcast_to(array[None], (length, *array.shape)), axi...  27.1 us
    all_to_all x1, blocking collectives, body(): lax.all_to_all(standard, 'row', split_axis=1, concat_axis=0, tiled=True)  25.6 us
    all_to_all x1, blocking collectives, body(): lax.all_to_all(standard, COL, split_axis=1, concat_axis=0, tiled=True)  18.3 us
    all_gather x1, blocking collectives, total_of_pieces(): return lax.all_gather(array, axis).sum(0)  15.7 us
  transfers between devices with their start and end apart: 4, of which 4 were waited for; matrix products, arithmetic and copies ran while one was open for 5% of the time, Pallas kernels for 0%

commit v1 on v0

--- a/solution.py
+++ b/solution.py
@@ -70,7 +70,9 @@
     row_piece = lax.all_to_all(standard, "row", split_axis=1, concat_axis=0, tiled=True)
     col_piece = lax.all_to_all(standard, COL, split_axis=1, concat_axis=0, tiled=True)
     col_piece = col_piece.reshape(col_count, 1, own_snps, col_piece.shape[1])
-    col_panel = lax.all_gather(col_piece, "row", axis=1, tiled=True)
+    col_panel = jnp.concatenate(
+        lax.all_to_all(jnp.stack([col_piece] * lax.axis_size("row")), "row", 0, 0), axis=1
+    )
     col_panel = col_panel.reshape(total_snps, col_panel.shape[3])
     window = lax.dot_general(
         lax.all_gather(row_piece, COL, axis=0, tiled=True),

time: 352 us -> 434 us (1.23)
  waiting for transfers between devices: 152 us -> 230 us
  starting transfers between devices: 0.35 us -> 6.45 us
    all_to_all x0 -> x1, waiting for transfers between devices: none -> 181 us  [body(): lax.all_to_all(jnp.stack([col_piece] * lax.axis_size('row')), 'row', 0, 0)]
    all_gather x1, waiting for transfers between devices: 63.9 us -> 0.01 us  [body(): lax.all_gather(row_piece, COL, axis=0, tiled=True)]
    all_gather x1 -> x0, waiting for transfers between devices: 37.5 us -> none  [body(): col_panel = lax.all_gather(col_piece, 'row', axis=1, tiled=True)]
    all_gather x1 -> x0, local copies, waits for them, and re-layouts: 11.3 us -> none  [body(): col_panel = lax.all_gather(col_piece, 'row', axis=1, tiled=True)]
    all_to_all x1, local copies, waits for them, and re-layouts: 1.08 us -> 8.52 us  [body(): lax.all_to_all(jnp.stack([col_piece] * lax.axis_size('row')), 'row', 0, 0)]
    all_to_all x0 -> x1, starting transfers between devices: none -> 6.33 us  [body(): lax.all_to_all(jnp.stack([col_piece] * lax.axis_size('row')), 'row', 0, 0)]
  transfers between devices with their start and end apart: 4 -> 4, of which waited for: 4 -> 3; matrix products, arithmetic and copies ran while one was open for 5% -> 3% of each run, Pallas kernels for 0% -> 0%
where the time goes in v1:
time: 434 us; the launch traced here: 433 us
  waiting for transfers between devices  230 us (53%)
  blocking collectives  117 us (27%)
  local copies, waits for them, and re-layouts  25 us (6%)
  matrix products  21.5 us (5%)
  other arithmetic  18.8 us (4%)
  between operations  13.9 us (3%)
  starting transfers between devices  6.45 us (1%)
    all_to_all x1, waiting for transfers between devices, body(): lax.all_to_all(jnp.stack([col_piece] * lax.axis_size('row')), 'row', 0, 0)  181 us
    all_gather x2, waiting for transfers between devices, total_of_pieces(): return lax.all_gather(array, axis).sum(0)  48.2 us
    psum x2, blocking collectives, one_axis_at_a_time(): array = lax.psum(array, axis)  33.6 us
    all_to_all x1, blocking collectives, copy_for_each(): lax.all_to_all(jnp.broadcast_to(array[None], (length, *array.shape)), axi...  27.1 us
    all_to_all x1, blocking collectives, body(): lax.all_to_all(standard, 'row', split_axis=1, concat_axis=0, tiled=True)  22.7 us
    all_to_all x1, blocking collectives, body(): lax.all_to_all(standard, COL, split_axis=1, concat_axis=0, tiled=True)  18.3 us
    all_gather x1, blocking collectives, total_of_pieces(): return lax.all_gather(array, axis).sum(0)  15.7 us
    dot_general x1, matrix products, body(): lax.dot_general(lax.all_gather(row_piece, COL, axis=0, tiled=True), col_p...  14.4 us
  transfers between devices with their start and end apart: 4, of which 3 were waited for; matrix products, arithmetic and copies ran while one was open for 3% of the time, Pallas kernels for 0%

profile of v1, /device:TPU:32, one launch (start us, length us, event | category | flops | bytes accessed | tf_op | source)
XLA Modules:
  0.0 433.5 jit_solution(18113665832175026828)
XLA Ops:
  9.3 1.4 divide_convert_fusion
  10.8 18.3 %all_to_all.43 = bf16[16,16,1024]{2,0,1:T(8,128)(2,1)S(1)} all-to-all(bf16[16,16,1024]{2,0,1:T(8,128)(2,1)S(1)} %bitcast.84), channel_id=1, replica_groups=mesh['row'=16,'col_0'=4,'col_1'=4] {'col_0','col_1'}, dimensions={1} | all-to-all | bytes 1048576 | tf_op jit(solution)/shard_map/all_to_all | solution.py:71
  29.1 22.7 %all_to_all.44 = bf16[16,16,1024]{2,0,1:T(8,128)(2,1)} all-to-all(bf16[16,16,1024]{2,0,1:T(8,128)(2,1)S(1)} %bitcast.85), channel_id=1, replica_groups=mesh['row'=16,'col_0'=4,'col_1'=4] {'row'}, dimensions={1} | all-to-all | bytes 1048576 | tf_op jit(solution)/shard_map/all_to_all | solution.py:70
  51.8 4.3 stack.15
  56.2 6.3 %all-to-all-start.2 = ((bf16[16,16,1,16,1024]{4,3,1,2,0:T(8,128)(2,1)}), bf16[16,16,1,16,1024]{4,3,1,2,0:T(8,128)(2,1)}, u32[]{:S(2)}, u32[]{:S(2)}) async-start(bf16[16,16,1,16,1024]{4,3,1,2,0:T(8,128)(2,1)} %stack.15), calls=%async_computation.2 | async-start | bytes 16777216 | tf_op jit(solution)/shard_map/all_to_all | solution.py:74
  63.3 181.5 %all-to-all-done.2 = bf16[16,16,1,16,1024]{4,3,1,2,0:T(8,128)(2,1)} async-done(((bf16[16,16,1,16,1024]{4,3,1,2,0:T(8,128)(2,1)}), bf16[16,16,1,16,1024]{4,3,1,2,0:T(8,128)(2,1)}, u32[]{:S(2)}, u32[]{:S(2)}) %all-to-all-start.2) | async-done | bytes 8388640 | tf_op jit(solution)/shard_map/all_to_all | solution.py:74
  244.7 8.5 %copy.43 = bf16[16,16,1,16,1024]{4,3,0,1,2:T(8,128)(2,1)} copy(bf16[16,16,1,16,1024]{4,3,1,2,0:T(8,128)(2,1)} %all-to-all-done.2) | data formatting | bytes 16777216 | tf_op jit(solution)/shard_map/all_to_all | solution.py:74
  253.3 14.4 %multiply_add_fusion = f32[1024,1024]{1,0:T(8,128)S(1)} fusion(f32[1024,1024]{1,0:T(8,128)} %param.11, bf16[4096,1024]{1,0:T(8,128)(2,1)} %all-gather.8.cloned.1.call-done, bf16[4096,1024]{1,0:T(8,128)(2,1)} %bitcast.81), kind=kOutput, calls=%fused_computation.4 | convolution fusion | flops 8592031744 | bytes 25165824 | tf_op jit(solution)/shard_map/dot_general | solution.py:77
  267.7 2.0 copy-done.1
  270.8 35.8 %all-gather.10.cloned.1.call-done = f32[16384,20]{0,1:T(8,128)} async-done(((f32[1024,20]{0,1:T(8,128)}), f32[16384,20]{0,1:T(8,128)}) %all-gather.10.cloned.1.call-update) | async-done | bytes 1310736 | tf_op jit(solution)/shard_map/all_gather | solution.py:14
  306.5 2.5 copy.56
  311.3 27.1 %all_to_all.45 = f32[16,1,20880]{2,1,0:T(1,128)S(1)} all-to-all(f32[16,1,20880]{2,1,0:T(1,128)S(1)} %broadcast_in_dim.22), channel_id=1, replica_groups=mesh['row'=16,'col_0'=4,'col_1'=4] {'col_0','col_1'}, dimensions={0} | all-to-all | bytes 2672640 | tf_op jit(solution)/shard_map/all_to_all | solution.py:19
  339.5 1.8 cholesky.59
  342.6 1.5 custom-call.13
  345.3 3.2 fusion.27
  348.7 15.7 %all-gather.3 = f32[16,20,20]{2,1,0:T(8,128)S(1)} all-gather(f32[1,20,20]{2,1,0:T(8,128)S(1)} %convolution_bitcast_fusion.3), channel_id=3, replica_groups=mesh['row'=16,'col_0'=4,'col_1'=4] {'row'}, dimensions={0}, use_global_device_ids=true | all-gather | bytes 27200 | tf_op jit(solution)/shard_map/all_gather | solution.py:14
  364.6 1.8 cholesky.70
  367.7 1.5 custom-call.14
  370.8 12.4 %all-gather.12.cloned.1.call-done = f32[16384,20]{0,1:T(8,128)} async-done(((f32[1024,20]{0,1:T(8,128)}), f32[16384,20]{0,1:T(8,128)}) %all-gather.12.cloned.1.call-update) | async-done | bytes 1310736 | tf_op jit(solution)/shard_map/all_gather | solution.py:14
  383.2 2.3 copy.57
  386.2 16.8 %psum.14 = f32[20,20]{0,1:T(8,128)S(1)} all-reduce(f32[20,20]{0,1:T(8,128)S(1)} %fusion.28), channel_id=1, replica_groups=mesh['row'=16,'col_0'=4,'col_1'=4] {'col_0'}, use_global_device_ids=true, to_apply=%region_6.9 | all-reduce | flops 400 | bytes 3200 | tf_op jit(solution)/shard_map/psum | solution.py:39
  403.0 16.8 %psum.15 = f32[20,20]{0,1:T(8,128)S(1)} all-reduce(f32[20,20]{0,1:T(8,128)S(1)} %psum.14), channel_id=1, replica_groups=mesh['row'=16,'col_0'=4,'col_1'=4] {'col_1'}, use_global_device_ids=true, to_apply=%region_7.10 | all-reduce | flops 400 | bytes 3200 | tf_op jit(solution)/shard_map/psum | solution.py:39
  419.9 1.8 cholesky.81
  423.9 1.5 custom-call.15
  (60 shorter events, 17.4 us)
Async XLA Ops:
  7.2 0.8 copy-start
  56.2 188.6 %all-to-all-start.2 = ((bf16[16,16,1,16,1024]{4,3,1,2,0:T(8,128)(2,1)}), bf16[16,16,1,16,1024]{4,3,1,2,0:T(8,128)(2,1)}, u32[]{:S(2)}, u32[]{:S(2)}) async-start(bf16[16,16,1,16,1024]{4,3,1,2,0:T(8,128)(2,1)} %stack.15), calls=%async_computation.2 | async-start | bytes 16777216 | tf_op jit(solution)/shard_map/all_to_all | solution.py:74
  62.5 190.8 %all-gather.8.cloned.1.call-start = ((), (), s32[]{:S(2)}) async-start(), calls=%async_computation.4 | async-start | bytes 8912896 | tf_op jit(solution)/shard_map/all_gather | solution.py:78
  63.2 243.3 %all-gather.10.cloned.1.call-start = ((), (), s32[]{:S(2)}) async-start(), calls=%async_computation.5 | async-start | bytes 1671168 | tf_op jit(solution)/shard_map/all_gather | solution.py:14
  253.3 16.4 %copy-start.3 = (f32[1024,20]{0,1:T(8,128)S(1)}, f32[1024,20]{0,1:T(8,128)}, u32[]{:S(2)}) copy-start(f32[1024,20]{0,1:T(8,128)} %param.12) | copy-start | bytes 245764
  267.7 2.0 copy-start.1
  270.7 112.5 %all-gather.12.cloned.1.call-start = ((), (), s32[]{:S(2)}) async-start(), calls=%async_computation.6 | async-start | bytes 1671168 | tf_op jit(solution)/shard_map/all_gather | solution.py:14
  306.5 2.7 copy-start.2
Sparse Core Ops, SparseCore 0:
  65.7 73.5 all-gather.7
  270.8 35.6 all-gather.9
  348.7 34.5 all-gather.11
